TPU v7x, 64 devices: a 2x2x8 block of a 4x4x8 slice. The times are simulated.
64 devices in a mesh: rep: 8 (over x, y, core), dp: 8 (over z).
Axes of the slice: x: 2, y: 2, z: 8, core: 2. Of those that a mesh axis runs over, the one named last changes fastest.
The devices are a block of a 4x4x8 slice.
Arguments:
- x: bfloat16 [64, 4096, 512], P(('rep', 'dp')), parts along dimension 0
- dy: bfloat16 [64, 4096, 512], P(('rep', 'dp')), parts along dimension 0
- w_gate: bfloat16 [2, 512, 2048], replicated
- w_up: bfloat16 [2, 512, 2048], replicated
- w_down: bfloat16 [2, 2048, 512], replicated
- m_w_gate: float32 [2, 512, 2048], replicated
- m_w_up: float32 [2, 512, 2048], replicated
- m_w_down: float32 [2, 2048, 512], replicated
- v_w_gate: float32 [2, 512, 2048], replicated
- v_w_up: float32 [2, 512, 2048], replicated
- v_w_down: float32 [2, 2048, 512], replicated
Outputs:
- output 1: bfloat16 [16, 512, 2048], P('rep'), parts along dimension 0
- output 2: bfloat16 [16, 512, 2048], P('rep'), parts along dimension 0
- output 3: bfloat16 [16, 2048, 512], P('rep'), parts along dimension 0
- output 4: float32 [16, 512, 2048], P('rep'), parts along dimension 0
- output 5: float32 [16, 512, 2048], P('rep'), parts along dimension 0
- output 6: float32 [16, 2048, 512], P('rep'), parts along dimension 0
- output 7: float32 [16, 512, 2048], P('rep'), parts along dimension 0
- output 8: float32 [16, 512, 2048], P('rep'), parts along dimension 0
- output 9: float32 [16, 2048, 512], P('rep'), parts along dimension 0
There are 8 independent parts. A program takes and returns all parts, laid end to end along the dimension named above; an argument that names none is the same for every part.
All inputs are finite; a program needn't handle non-finite values.
Results may differ from a plain program's by a relative error of at most 0.02.
Values are sent between devices in bfloat16 or wider.
A program may use at most 768 MiB of HBM per device.

v0:
```python
import jax
import jax.numpy as jnp
from jax import lax
from jax.sharding import PartitionSpec as P

NAMES = ("w_gate", "w_up", "w_down")


def matmul(a, w):
    return jnp.dot(a, w, preferred_element_type=jnp.float32).astype(jnp.bfloat16)


def normed(h):
    wide = h.astype(jnp.float32)
    scale = lax.rsqrt(jnp.mean(wide**2, -1, keepdims=True) + 1e-6)
    return (wide * scale).astype(jnp.bfloat16)


def layer(h, w):
    a = normed(h)
    gate = jnp.dot(a, w["w_gate"], preferred_element_type=jnp.float32)
    up = jnp.dot(a, w["w_up"], preferred_element_type=jnp.float32)
    return h + matmul((jax.nn.silu(gate) * up).astype(jnp.bfloat16), w["w_down"])


def adamw(w, m, v, g):
    m = 0.9 * m + 0.1 * g
    v = 0.95 * v + 0.05 * g * g
    step = m * lax.rsqrt(v + 1e-8) + 0.1 * w
    return (w - 0.02 * step).astype(jnp.bfloat16), m, v


def solution(mesh):
    def step(x, dy, *arrays):
        weights, m, v = (arrays[i : i + 3] for i in (0, 3, 6))
        layers = weights[0].shape[0]
        h, kept = x[0], []
        for number in range(layers):
            kept.append(h)
            h = layer(h, {name: w[number] for name, w in zip(NAMES, weights, strict=True)})
        by_h, summed = dy[0], [None] * layers
        for number in reversed(range(layers)):
            _, back = jax.vjp(lambda w, h: layer(h, w), {name: w[number] for name, w in zip(NAMES, weights, strict=True)}, kept[number])
            by_w, by_h = back(by_h)
            summed[number] = [lax.psum(by_w[name], "dp") for name in NAMES]
        gradients = [jnp.stack([summed[number][i] for number in range(layers)]).astype(jnp.float32) for i in range(3)]
        new = [adamw(w.astype(jnp.float32), m, v, g) for w, m, v, g in zip(weights, m, v, gradients, strict=True)]
        return tuple(one[which] for which in range(3) for one in new)

    return jax.shard_map(
        step,
        mesh=mesh,
        in_specs=(P(("rep", "dp"), None, None),) * 2 + (P(None, None, None),) * 9,
        out_specs=(P("rep", None, None),) * 9,
        check_vma=False,
    )
```

profile of v0, /device:TPU:21, one launch (start us, length us, event | category | flops | bytes accessed | tf_op | source)
XLA Modules:
  0.0 668.3 jit_solution(14003561482113259172)
XLA Ops:
  7.2 0.1 all-reduce.3.cloned.1.call-start
  7.3 6.3 copy.20
  13.6 3.1 fusion.18
  16.7 6.3 copy.21
  23.0 15.1 %convolution_convert_fusion.1 = bf16[4096,2048]{1,0:T(8,128)(2,1)} fusion(bf16[1,4096,512]{2,1,0:T(8,128)(2,1)} %param.12, bf16[2,2048,512]{2,1,0:T(8,128)(2,1)} %param.15), kind=kOutput, calls=%fused_computation.25 | convolution fusion | flops 8598323200 | bytes 23068672 | tf_op jit(solution)/shard_map/transpose(jvp())/dot_general | solution.py:10
  38.1 17.8 %fusion.88 = f32[4096,2048]{1,0:T(8,128)} fusion(bf16[2,512,2048]{2,1,0:T(8,128)(2,1)S(1)} %copy-done.2, bf16[1,4096,512]{2,1,0:T(8,128)(2,1)} %param.11, f32[4096]{0:T(1024)S(1)} %add_rsqrt_fusion), kind=kOutput, calls=%fused_computation.103 | convolution fusion | flops 8596226048 | bytes 39862272 | tf_op jit(solution)/shard_map/dot_general | solution.py:21
  55.9 32.5 %multiply_convert_fusion.1 = (bf16[4096,2048]{1,0:T(8,128)(2,1)}, f32[4096,2048]{1,0:T(8,128)}) fusion(f32[4096,2048]{1,0:T(8,128)} %fusion.88, bf16[2,512,2048]{2,1,0:T(8,128)(2,1)S(1)} %copy-done.5, bf16[1,4096,512]{2,1,0:T(8,128)(2,1)} %param.11, f32[4096]{0:T(1024)S(1)} %add_rsqrt_fusion), kind=kOutput, calls=%fused_computation.17 | convolution fusion | flops 8646557696 | bytes 90193920 | tf_op jit(solution)/shard_map/dot_general | solution.py:22
  88.4 15.8 %fusion.34 = (f32[4096]{0:T(1024)S(1)}, bf16[4096,512]{0,1:T(8,128)(2,1)}) fusion(bf16[4096,2048]{1,0:T(8,128)(2,1)} %get-tuple-element.24, bf16[2,2048,512]{2,1,0:T(8,128)(2,1)} %param.15, bf16[1,4096,512]{1,2,0:T(8,128)(2,1)} %copy.20), kind=kOutput, calls=%fused_computation.64 | convolution fusion | flops 8600416256 | bytes 27279360 | tf_op jit(solution)/shard_map/dot_general | solution.py:10
  104.2 18.2 %fusion.75 = f32[4096,2048]{1,0:T(8,128)} fusion(bf16[4096,512]{0,1:T(8,128)(2,1)} %get-tuple-element.27, f32[4096]{0:T(1024)S(1)} %fusion.101, bf16[2,512,2048]{2,1,0:T(8,128)(2,1)} %param.14), kind=kOutput, calls=%fused_computation.92 | convolution fusion | flops 8596226048 | bytes 39862272 | tf_op jit(solution)/shard_map/jvp()/dot_general | solution.py:22
  122.4 41.0 %fusion.2 = (bf16[4096,2048]{1,0:T(8,128)(2,1)}, f32[4096,2048]{1,0:T(8,128)}) fusion(f32[4096,2048]{1,0:T(8,128)} %fusion.75, bf16[4096,2048]{1,0:T(8,128)(2,1)} %convolution_convert_fusion.1, bf16[2,512,2048]{2,1,0:T(8,128)(2,1)} %param.13, bf16[4096,512]{0,1:T(8,128)(2,1)} %get-tuple-element.27, f32[4096]{0:T(1024)S(1)} %fusion.101), kind=kOutput, calls=%fused_computation.8 | convolution fusion | flops 8696889344 | bytes 106971136 | tf_op jit(solution)/shard_map/jvp()/dot_general | solution.py:21
  163.4 26.0 %fusion.59 = bf16[1,2048,512]{2,1,0:T(8,128)(2,1)} fusion(bf16[1,4096,512]{2,1,0:T(8,128)(2,1)} %param.12, f32[4096,2048]{1,0:T(8,128)} %fusion.75, f32[4096,2048]{1,0:T(8,128)} %get-tuple-element.29), kind=kOutput, calls=%fused_computation.86 | convolution fusion | flops 8641314816 | bytes 73400320 | tf_op jit(solution)/shard_map/transpose(jvp())/dot_general | solution.py:10
  189.3 20.6 %fusion.62 = bf16[1,512,2048]{2,1,0:T(8,128)(2,1)} fusion(bf16[4096,2048]{1,0:T(8,128)(2,1)} %convolution_convert_fusion.1, bf16[4096,512]{0,1:T(8,128)(2,1)S(1)} %copy-done.7, f32[4096]{0:T(1024)S(1)} %fusion.101, f32[4096,2048]{1,0:T(8,128)} %get-tuple-element.29), kind=kOutput, calls=%fused_computation.87 | convolution fusion | flops 8647606272 | bytes 56639488 | tf_op jit(solution)/shard_map/transpose(jvp())/dot_general | solution.py:22
  209.9 21.8 %fusion.37 = bf16[4096,512]{0,1:T(8,128)(2,1)} fusion(bf16[4096,2048]{1,0:T(8,128)(2,1)} %convolution_convert_fusion.1, bf16[2,512,2048]{2,1,0:T(8,128)(2,1)} %param.14, f32[4096,2048]{1,0:T(8,128)} %get-tuple-element.29), kind=kOutput, calls=%fused_computation.68 | convolution fusion | flops 8642363392 | bytes 56623104 | tf_op jit(solution)/shard_map/transpose(jvp())/dot_general | solution.py:22
  231.7 14.9 %fusion.63 = bf16[1,512,2048]{2,1,0:T(8,128)(2,1)} fusion(bf16[4096,2048]{1,0:T(8,128)(2,1)} %get-tuple-element.28, bf16[4096,512]{0,1:T(8,128)(2,1)} %get-tuple-element.27, f32[4096]{0:T(1024)S(1)} %fusion.101), kind=kOutput, calls=%fused_computation.88 | convolution fusion | flops 8596226048 | bytes 23085056 | tf_op jit(solution)/shard_map/transpose(jvp())/dot_general | solution.py:21
  246.6 15.1 %fusion.36 = (f32[4096]{0:T(1024)S(1)}, bf16[4096,512]{0,1:T(8,128)(2,1)}) fusion(bf16[4096,512]{0,1:T(8,128)(2,1)S(1)} %copy-done.8, bf16[4096,512]{0,1:T(8,128)(2,1)} %fusion.37, bf16[4096,2048]{1,0:T(8,128)(2,1)} %get-tuple-element.28, bf16[2,512,2048]{2,1,0:T(8,128)(2,1)S(1)} %copy-done.3), kind=kOutput, calls=%fused_computation.66 | convolution fusion | flops 8600416256 | bytes 31473664 | tf_op jit(solution)/shard_map/transpose(jvp())/dot_general | solution.py:21
  261.7 4.3 fusion.42
  266.0 2.0 copy-done.9
  268.1 13.8 %fusion.64 = bf16[1,2048,512]{2,1,0:T(8,128)(2,1)} fusion(bf16[4096,2048]{1,0:T(8,128)(2,1)} %get-tuple-element.24, bf16[4096,512]{0,1:T(8,128)(2,1)S(1)} %fusion.42), kind=kOutput, calls=%fused_computation.89 | convolution fusion | flops 8590983168 | bytes 23068672 | tf_op jit(solution)/shard_map/transpose(jvp())/dot_general | solution.py:10
  281.9 14.8 %convolution_convert_fusion = bf16[4096,2048]{1,0:T(8,128)(2,1)} fusion(bf16[4096,512]{0,1:T(8,128)(2,1)} %copy-done.9, bf16[2,2048,512]{2,1,0:T(8,128)(2,1)S(1)} %copy-done.10), kind=kOutput, calls=%fused_computation.24 | convolution fusion | flops 8598323200 | bytes 23068672 | tf_op jit(solution)/shard_map/transpose(jvp())/dot_general | solution.py:10
  296.7 20.8 %fusion.65 = bf16[1,512,2048]{2,1,0:T(8,128)(2,1)} fusion(bf16[4096,2048]{1,0:T(8,128)(2,1)} %convolution_convert_fusion, f32[4096,2048]{1,0:T(8,128)} %fusion.88, bf16[1,4096,512]{1,2,0:T(8,128)(2,1)S(1)} %copy-done, f32[4096]{0:T(1024)S(1)} %copy-done.14), kind=kOutput, calls=%fused_computation.90 | convolution fusion | flops 8647606272 | bytes 56639488 | tf_op jit(solution)/shard_map/transpose(jvp())/dot_general | solution.py:22
  317.5 34.0 %fusion.68 = bf16[1,512,2048]{2,1,0:T(8,128)(2,1)} fusion(f32[4096,2048]{1,0:T(8,128)} %fusion.88, f32[4096,2048]{1,0:T(8,128)} %get-tuple-element.25, bf16[4096,2048]{1,0:T(8,128)(2,1)} %convolution_convert_fusion, bf16[1,4096,512]{1,2,0:T(8,128)(2,1)} %copy.20, f32[4096]{0:T(1024)S(1)} %copy-done.14), kind=kOutput, calls=%fused_computation.91 | convolution fusion | flops 8689549312 | bytes 90193920 | tf_op jit(solution)/shard_map/transpose(jvp())/dot_general | solution.py:21
  351.5 264.9 %all-reduce.3.cloned.1.call-done = (bf16[1,512,2048]{2,1,0:T(8,128)(2,1)}, bf16[1,512,2048]{2,1,0:T(8,128)(2,1)}, bf16[1,512,2048]{2,1,0:T(8,128)(2,1)}, bf16[1,...) async-done(((bf16[1,512,2048]{2,1,0:T(8,128)(2,1)}, bf16[1,512,2048]{2,1,0:T(8,128)(2,1)}, bf16[1,512,2048]{2,1,0:T(8,128)(2,1)}, ...) | async-done | bytes 12582928 | tf_op jit(solution)/shard_map/psum | solution.py:45
  616.5 16.7 %fusion.29 = (bf16[2,2048,512]{2,1,0:T(8,128)(2,1)}, f32[2,2048,512]{2,1,0:T(8,128)}, f32[2,2048,512]{2,1,0:T(8,128)}) fusion(bf16[2,2048,512]{2,1,0:T(8,128)(2,1)} %param.15, bf16[1,2048,512]{2,1,0:T(8,128)(2,1)} %get-tuple-element.13, bf16[1,2048,512]{2,1,0:T(8,128)(2,1)} %get-tuple-element.14, f32[2,2048,512]{2,1,0:T(8,128)} %param.21, ...), kind=kLoop, calls=%fused_computation.59 | loop fusion | flops 39845888 | bytes 46137344 | tf_op jit(solution)/shard_map/convert_element_type | solution.py:30
  633.2 27.7 %fusion.17 = (bf16[2,512,2048]{2,1,0:T(8,128)(2,1)}, f32[2,512,2048]{2,1,0:T(8,128)}, f32[2,512,2048]{2,1,0:T(8,128)}, bf16[2,512,2048]{2,1,0:T(8,128)(2,1)}, f3...) fusion(bf16[2,512,2048]{2,1,0:T(8,128)(2,1)S(1)} %copy-done.4, bf16[1,512,2048]{2,1,0:T(8,128)(2,1)} %get-tuple-element.9, ...), kind=kLoop, calls=%fused_computation.47 | loop fusion | flops 79691776 | bytes 92274688 | tf_op jit(solution)/shard_map/convert_element_type | solution.py:30
  (33 shorter events, 0.2 us)
Async XLA Ops:
  7.2 609.3 %all-reduce.3.cloned.1.call-start = ((), (), s32[]{:S(2)}) async-start(), calls=%async_computation | async-start | bytes 25165824 | tf_op jit(solution)/shard_map/psum | solution.py:45
  16.7 39.2 %copy-start.13 = (f32[4096]{0:T(1024)}, f32[4096]{0:T(1024)S(1)}, u32[]{:S(2)}) copy-start(f32[4096]{0:T(1024)S(1)} %add_rsqrt_fusion) | copy-start | bytes 49156
  23.0 15.1 %copy-start.2 = (bf16[2,512,2048]{2,1,0:T(8,128)(2,1)S(1)}, bf16[2,512,2048]{2,1,0:T(8,128)(2,1)}, u32[]{:S(2)}) copy-start(bf16[2,512,2048]{2,1,0:T(8,128)(2,1)} %param.13) | copy-start | bytes 12582916
  38.1 17.8 %copy-start.5 = (bf16[2,512,2048]{2,1,0:T(8,128)(2,1)S(1)}, bf16[2,512,2048]{2,1,0:T(8,128)(2,1)}, u32[]{:S(2)}) copy-start(bf16[2,512,2048]{2,1,0:T(8,128)(2,1)} %param.14) | copy-start | bytes 12582916
  104.2 18.2 %copy-start.11 = (f32[4096]{0:T(1024)}, f32[4096]{0:T(1024)S(1)}, u32[]{:S(2)}) copy-start(f32[4096]{0:T(1024)S(1)} %get-tuple-element.26) | copy-start | bytes 49156
  163.4 26.0 %copy-start.7 = (bf16[4096,512]{0,1:T(8,128)(2,1)S(1)}, bf16[4096,512]{0,1:T(8,128)(2,1)}, u32[]{:S(2)}) copy-start(bf16[4096,512]{0,1:T(8,128)(2,1)} %get-tuple-element.27) | copy-start | bytes 12582916
  231.7 14.9 %copy-start.3 = (bf16[2,512,2048]{2,1,0:T(8,128)(2,1)S(1)}, bf16[2,512,2048]{2,1,0:T(8,128)(2,1)}, u32[]{:S(2)}) copy-start(bf16[2,512,2048]{2,1,0:T(8,128)(2,1)} %param.13) | copy-start | bytes 12582916
  231.7 14.9 %copy-start.8 = (bf16[4096,512]{0,1:T(8,128)(2,1)S(1)}, bf16[4096,512]{0,1:T(8,128)(2,1)}, u32[]{:S(2)}) copy-start(bf16[4096,512]{0,1:T(8,128)(2,1)} %get-tuple-element.27) | copy-start | bytes 12582916
  246.6 15.1 %copy-start.12 = (f32[4096]{0:T(1024)S(1)}, f32[4096]{0:T(1024)}, u32[]{:S(2)}) copy-start(f32[4096]{0:T(1024)} %copy-done.11) | copy-start | bytes 49156
  246.6 15.1 %copy-start.1 = (bf16[1,4096,512]{1,2,0:T(8,128)(2,1)S(1)}, bf16[1,4096,512]{1,2,0:T(8,128)(2,1)}, u32[]{:S(2)}) copy-start(bf16[1,4096,512]{1,2,0:T(8,128)(2,1)} %copy.21) | copy-start | bytes 12582916
  266.0 2.0 copy-start.9
  268.0 13.8 %copy-start.10 = (bf16[2,2048,512]{2,1,0:T(8,128)(2,1)S(1)}, bf16[2,2048,512]{2,1,0:T(8,128)(2,1)}, u32[]{:S(2)}) copy-start(bf16[2,2048,512]{2,1,0:T(8,128)(2,1)} %param.15) | copy-start | bytes 12582916
  281.8 14.8 %copy-start = (bf16[1,4096,512]{1,2,0:T(8,128)(2,1)S(1)}, bf16[1,4096,512]{1,2,0:T(8,128)(2,1)}, u32[]{:S(2)}) copy-start(bf16[1,4096,512]{1,2,0:T(8,128)(2,1)} %copy.20) | copy-start | bytes 12582916
  281.8 14.8 %copy-start.14 = (f32[4096]{0:T(1024)S(1)}, f32[4096]{0:T(1024)}, u32[]{:S(2)}) copy-start(f32[4096]{0:T(1024)} %copy-done.13) | copy-start | bytes 49156
  616.5 16.7 %copy-start.4 = (bf16[2,512,2048]{2,1,0:T(8,128)(2,1)S(1)}, bf16[2,512,2048]{2,1,0:T(8,128)(2,1)}, u32[]{:S(2)}) copy-start(bf16[2,512,2048]{2,1,0:T(8,128)(2,1)} %param.13) | copy-start | bytes 12582916
  616.5 16.7 %copy-start.6 = (bf16[2,512,2048]{2,1,0:T(8,128)(2,1)S(1)}, bf16[2,512,2048]{2,1,0:T(8,128)(2,1)}, u32[]{:S(2)}) copy-start(bf16[2,512,2048]{2,1,0:T(8,128)(2,1)} %param.14) | copy-start | bytes 12582916
Sparse Core Ops, SparseCore 0:
  351.7 264.7 all-reduce.2
where the time goes:
time: 676 us; the launch traced here: 668 us
  matrix products  322 us (48%)
  waiting for transfers between devices  265 us (39%)
  other arithmetic  51.8 us (8%)
  local copies, waits for them, and re-layouts  14.7 us (2%)
  between operations  14.7 us (2%)
    psum x1, waiting for transfers between devices, step(): summed[number] = [lax.psum(by_w[name], 'dp') for name in NAMES]  265 us
    dot_general x5, matrix products, layer(): gate = jnp.dot(a, w['w_gate'], preferred_element_type=jnp.float32)  123 us
    dot_general x5, matrix products, layer(): up = jnp.dot(a, w['w_up'], preferred_element_type=jnp.float32)  114 us
    dot_general x5, matrix products, matmul(): jnp.dot(a, w, preferred_element_type=jnp.float32).astype(jnp.bfloat16)  85.5 us
    convert_element_type x2, other arithmetic, adamw(): return ((w - 0.02 * step).astype(jnp.bfloat16), m, v)  44.4 us
    unnamed x32, local copies, waits for them, and re-layouts  14.7 us
  transfers between devices with their start and end apart: 1, of which 1 were waited for; matrix products, arithmetic and copies ran while one was open for 0% of the time, Pallas kernels for 0%

commit v1 on v0

v1 whole, which is shorter than its diff:
```python
import functools

import jax
import jax.numpy as jnp
from jax import lax
from jax.experimental import pallas as pl
from jax.experimental.pallas import tpu as pltpu
from jax.sharding import PartitionSpec as P

F32, BF16 = jnp.float32, jnp.bfloat16
FB = 256
FTM = 512
TM = 1024
VMEM_LIMIT = 64 * 1024 * 1024 - 64 * 1024


def dot(a, b):
    return jnp.dot(a, b, preferred_element_type=F32)


def dot_nt(a, b):
    return lax.dot_general(a, b, (((1,), (1,)), ((), ())), preferred_element_type=F32)


def scale_of(wide):
    return lax.rsqrt(jnp.mean(wide * wide, -1, keepdims=True) + 1e-6)


def normed(h):
    wide = h.astype(F32)
    return (wide * scale_of(wide)).astype(BF16)


def sigmoid(x):
    return 1.0 / (1.0 + jnp.exp(-x))


def at(index, size):
    return pl.ds(pl.multiple_of(index * size, size), size)


def fetch(layer, sources, refs, sem):
    copies = [pltpu.make_async_copy(source.at[layer], ref, sem.at[k]) for k, (source, ref) in enumerate(zip(sources, refs, strict=True))]
    for copy in copies:
        copy.start()
    return copies


def forward_kernel(x_ref, wg_all, wu_all, wd_all, h_ref, wg_ref, wu_ref, wd_ref, sem, prod_ref):
    tokens, ff = x_ref.shape[0], wg_ref.shape[1]
    for copy in fetch(0, (wg_all, wu_all, wd_all), (wg_ref, wu_ref, wd_ref), sem):
        copy.wait()

    def tile(i, _):
        rows = at(i, FTM)
        x = x_ref[rows, :]
        a = normed(x)
        for c in range(0, ff, 512):
            gate = dot(a, wg_ref[:, c : c + 512])
            up = dot(a, wu_ref[:, c : c + 512])
            prod_ref[:, c : c + 512] = (gate * sigmoid(gate) * up).astype(BF16)
        y = dot(prod_ref[...], wd_ref[...]).astype(BF16)
        h_ref[rows, :] = (x.astype(F32) + y.astype(F32)).astype(BF16)
        return _

    lax.fori_loop(0, tokens // FTM, tile, 0)


def grads_loop(a_ref, at_ref, d_ref, dt_ref, wg_ref, wu_ref, wd_ref, da_ref, g_ref, prod_ref, dgate_ref, dup_ref, acc_ref):
    tokens, ff = a_ref.shape[0], wg_ref.shape[1]
    tiles = tokens // TM
    steps = (ff // FB) * tiles

    def first(t):
        j, i, slot = t // tiles, t % tiles, t % 2
        rows, cols = at(i, TM), at(j, FB)
        a, d = a_ref[rows, :], d_ref[rows, :]
        gate = dot(a, wg_ref[:, cols])
        up = dot(a, wu_ref[:, cols])
        dprod = dot_nt(d, wd_ref[cols, :]).astype(BF16).astype(F32)
        sig = sigmoid(gate)
        silu = gate * sig
        prod_ref[slot] = (silu * up).astype(BF16)
        dup_ref[slot] = (dprod * silu).astype(BF16)
        dgate_ref[slot] = (dprod * up * (sig * (1.0 + gate * (1.0 - sig)))).astype(BF16)

    def second(t):
        j, i, slot = t // tiles, t % tiles, t % 2
        rows, cols = at(i, TM), at(j, FB)
        fresh = i == 0
        dt, a_t = dt_ref[:, rows], at_ref[:, rows]
        prod, dgate, dup = prod_ref[slot], dgate_ref[slot], dup_ref[slot]
        for k, (left, right) in enumerate(((dt, prod), (a_t, dgate), (a_t, dup))):
            acc_ref[k] = jnp.where(fresh, 0.0, acc_ref[k]) + dot(left, right)
        if da_ref is not None:
            da = dot_nt(dgate, wg_ref[:, cols]) + dot_nt(dup, wu_ref[:, cols])
            da_ref[rows, :] = jnp.where(j == 0, 0.0, da_ref[rows, :]) + da

        @pl.when(i == tiles - 1)
        def _():
            d = g_ref.shape[2]
            for n in range(0, acc_ref.shape[1], d):
                g_ref[j, n : n + d, :] = acc_ref[0, n : n + d, :].T.astype(BF16)
            half = acc_ref.shape[1]
            g_ref[j, half : 2 * half, :] = acc_ref[1].astype(BF16)
            g_ref[j, 2 * half :, :] = acc_ref[2].astype(BF16)

    first(0)

    def step(t, _):
        first(t)
        second(t - 1)
        return _

    lax.fori_loop(1, steps, step, 0)
    second(steps - 1)


def last_layer_kernel(h_ref, dy_ref, wg_all, wu_all, wd_all, da_ref, g_ref, wg_ref, wu_ref, wd_ref, sem, a_ref, at_ref, dt_ref, *scratch):
    copies = fetch(1, (wg_all, wu_all, wd_all), (wg_ref, wu_ref, wd_ref), sem)

    def tile(i, _):
        rows = at(i, FTM)
        a = normed(h_ref[rows, :])
        a_ref[rows, :] = a
        at_ref[:, rows] = a.T
        dt_ref[:, rows] = dy_ref[rows, :].T
        return _

    lax.fori_loop(0, h_ref.shape[0] // FTM, tile, 0)
    for copy in copies:
        copy.wait()
    grads_loop(a_ref, at_ref, dy_ref, dt_ref, wg_ref, wu_ref, wd_ref, da_ref, g_ref, *scratch)


def first_layer_kernel(x_ref, h_ref, dy_ref, da_ref, wg_all, wu_all, wd_all, g_ref, wg_ref, wu_ref, wd_ref, sem, a_ref, at_ref, d_ref, dt_ref, *scratch):
    copies = fetch(0, (wg_all, wu_all, wd_all), (wg_ref, wu_ref, wd_ref), sem)

    def tile(i, _):
        rows = at(i, FTM)
        a = normed(x_ref[rows, :])
        a_ref[rows, :] = a
        at_ref[:, rows] = a.T
        wide = h_ref[rows, :].astype(F32)
        scale = scale_of(wide)
        da = da_ref[rows, :].astype(BF16).astype(F32)
        inner = jnp.mean(da * wide, -1, keepdims=True)
        dh = (scale * da - wide * (scale * scale * scale * inner)).astype(BF16)
        d = (dy_ref[rows, :].astype(F32) + dh.astype(F32)).astype(BF16)
        d_ref[rows, :] = d
        dt_ref[:, rows] = d.T
        return _

    lax.fori_loop(0, x_ref.shape[0] // FTM, tile, 0)
    for copy in copies:
        copy.wait()
    grads_loop(a_ref, at_ref, d_ref, dt_ref, wg_ref, wu_ref, wd_ref, None, g_ref, *scratch)


def grads_scratch(d):
    return [
        pltpu.VMEM((2, TM, FB), BF16),
        pltpu.VMEM((2, TM, FB), BF16),
        pltpu.VMEM((2, TM, FB), BF16),
        pltpu.VMEM((3, d, FB), F32),
    ]


def adam_kernel(g_ref, *refs):
    ins, outs = refs[:9], refs[-9:]
    d = ins[0].shape[0]
    fb = g_ref.shape[1]
    for k in range(3):
        w_ref, m_ref, v_ref = ins[k], ins[3 + k], ins[6 + k]
        ow, om, ov = outs[k], outs[3 + k], outs[6 + k]
        if k < 2:
            pieces = [((slice(None), slice(None)), slice(d + k * d, d + (k + 1) * d))]
        else:
            pieces = [((slice(None), slice(n, n + fb)), slice(n, n + fb)) for n in range(0, d, fb)]
        for place, rows in pieces:
            g = g_ref[rows, :].astype(F32)
            m = 0.9 * m_ref[place] + 0.1 * g
            v = 0.95 * v_ref[place] + 0.05 * g * g
            w = w_ref[place].astype(F32)
            ow[place] = (w - 0.02 * (m * lax.rsqrt(v + 1e-8) + 0.1 * w)).astype(BF16)
            om[place] = m
            ov[place] = v


def adam(layer, g, weights, moments, into):
    layers, d, ff = weights[0].shape
    wide = pl.BlockSpec((None, d, FB), lambda j: (layer, 0, j))
    tall = pl.BlockSpec((None, FB, d), lambda j: (layer, j, 0))
    specs = [wide, wide, tall] * 3
    arrays = [*weights, *moments]
    out_shape = [jax.ShapeDtypeStruct(a.shape, a.dtype) for a in arrays]
    extra = [] if into is None else list(into)
    return pl.pallas_call(
        adam_kernel,
        grid=(ff // FB,),
        out_shape=out_shape,
        in_specs=[pl.BlockSpec((None, *g.shape[1:]), lambda j: (j, 0, 0)), *specs, *[pl.BlockSpec(memory_space=pl.ANY)] * len(extra)],
        out_specs=specs,
        input_output_aliases={10 + k: k for k in range(len(extra))},
        cost_estimate=pl.CostEstimate(flops=60 * d * ff, bytes_accessed=3 * 22 * d * ff, transcendentals=3 * d * ff),
        compiler_params=pltpu.CompilerParams(vmem_limit_bytes=40 * 1024 * 1024),
        name="adam",
    )(g, *arrays, *extra)


def solution(mesh):
    def step(x, dy, *arrays):
        weights, moments = arrays[:3], arrays[3:]
        layers, d, ff = weights[0].shape
        x, dy = x[0], dy[0]
        tokens = x.shape[0]
        blocks = ff // FB
        whole = pl.BlockSpec(memory_space=pltpu.VMEM)

        any3 = [pl.BlockSpec(memory_space=pl.ANY)] * 3
        held = [pltpu.VMEM((d, ff), BF16), pltpu.VMEM((d, ff), BF16), pltpu.VMEM((ff, d), BF16), pltpu.SemaphoreType.DMA((3,))]

        params = pltpu.CompilerParams(vmem_limit_bytes=VMEM_LIMIT)
        flops = 2 * tokens * d * ff
        g_shape = jax.ShapeDtypeStruct((blocks, 3 * d, FB), BF16)
        h = pl.pallas_call(
            forward_kernel,
            out_shape=jax.ShapeDtypeStruct((tokens, d), BF16),
            in_specs=[whole, *any3],
            out_specs=whole,
            scratch_shapes=[*held, pltpu.VMEM((FTM, ff), BF16)],
            cost_estimate=pl.CostEstimate(flops=3 * flops, bytes_accessed=0, transcendentals=0),
            compiler_params=params,
            name="forward",
        )(x, *weights)
        da, g1 = pl.pallas_call(
            last_layer_kernel,
            out_shape=[jax.ShapeDtypeStruct((tokens, d), F32), g_shape],
            in_specs=[whole, whole, *any3],
            out_specs=[whole, whole],
            scratch_shapes=[*held, pltpu.VMEM((tokens, d), BF16), pltpu.VMEM((d, tokens), BF16), pltpu.VMEM((d, tokens), BF16), *grads_scratch(d)],
            cost_estimate=pl.CostEstimate(flops=8 * flops, bytes_accessed=0, transcendentals=0),
            compiler_params=params,
            name="last_layer",
        )(h, dy, *weights)
        s1 = lax.psum(g1, "dp")
        g0 = pl.pallas_call(
            first_layer_kernel,
            out_shape=g_shape,
            in_specs=[whole] * 4 + any3,
            out_specs=whole,
            scratch_shapes=[
                *held,
                pltpu.VMEM((tokens, d), BF16),
                pltpu.VMEM((d, tokens), BF16),
                pltpu.VMEM((tokens, d), BF16),
                pltpu.VMEM((d, tokens), BF16),
                *grads_scratch(d),
            ],
            cost_estimate=pl.CostEstimate(flops=6 * flops, bytes_accessed=0, transcendentals=0),
            compiler_params=params,
            name="first_layer",
        )(x, h, dy, da, *weights)
        g0, s1 = lax.optimization_barrier((g0, s1))
        s0 = lax.psum(g0, "dp")
        new = adam(1, s1, weights, moments, None)
        return tuple(adam(0, s0, weights, moments, new))

    return jax.shard_map(
        step,
        mesh=mesh,
        in_specs=(P(("rep", "dp"), None, None),) * 2 + (P(None, None, None),) * 9,
        out_specs=(P("rep", None, None),) * 9,
        check_vma=False,
    )
```

time: 676 us -> 468 us (0.69); the launches traced: 668 us -> 467 us
  matrix products: 322 us -> 0 us
  Pallas kernels: 0 us -> 262 us
  waiting for transfers between devices: 265 us -> 178 us
  other arithmetic: 51.8 us -> 0 us
    dot_general x15 -> x0, matrix products: 322 us -> none  [the longest x5 123 us: layer(): gate = jnp.dot(a, w['w_gate'], preferred_element_type=jnp.float32)]
    pallas_call x0 -> x5, Pallas kernels: none -> 262 us  [the longest x1 96.1 us: step(): pl.pallas_call(last_layer_kernel, out_shape=[jax.ShapeDtypeStruct((tokens...]
    psum x1 -> x2, waiting for transfers between devices: 265 us -> 178 us  [the longest x1 113 us: step(): s0 = lax.psum(g0, 'dp')]
    convert_element_type x2 -> x0, other arithmetic: 44.4 us -> none  [adamw(): return ((w - 0.02 * step).astype(jnp.bfloat16), m, v)]
    unnamed x32 -> x12, local copies, waits for them, and re-layouts: 14.7 us -> 13.1 us
  transfers between devices with their start and end apart: 1 -> 2, of which waited for: 1 -> 2; matrix products, arithmetic and copies ran while one was open for 0% -> 0% of each run, Pallas kernels for 0% -> 22%
where the time goes in v1:
time: 468 us; the launch traced here: 467 us
  Pallas kernels  262 us (56%)
  waiting for transfers between devices  178 us (38%)
  between operations  14.2 us (3%)
  local copies, waits for them, and re-layouts  13.1 us (3%)
    psum x1, waiting for transfers between devices, step(): s0 = lax.psum(g0, 'dp')  113 us
    pallas_call x1, Pallas kernels, step(): pl.pallas_call(last_layer_kernel, out_shape=[jax.ShapeDtypeStruct((tokens...  96.1 us
    pallas_call x1, Pallas kernels, step(): pl.pallas_call(first_layer_kernel, out_shape=g_shape, in_specs=[whole] *...  81.5 us
    psum x1, waiting for transfers between devices, step(): s1 = lax.psum(g1, 'dp')  64.5 us
    pallas_call x2, Pallas kernels, adam(): pl.pallas_call(adam_kernel, grid=(ff // FB,), out_shape=out_shape, in_spe...  46.3 us
    pallas_call x1, Pallas kernels, step(): pl.pallas_call(forward_kernel, out_shape=jax.ShapeDtypeStruct((tokens, d)...  38.1 us
    unnamed x12, local copies, waits for them, and re-layouts  13.1 us
  transfers between devices with their start and end apart: 2, of which 2 were waited for; matrix products, arithmetic and copies ran while one was open for 0% of the time, Pallas kernels for 22%

profile of v1, /device:TPU:21, one launch (start us, length us, event | category | flops | bytes accessed | tf_op | source)
XLA Modules:
  0.0 467.4 jit_solution(12371245454907809211)
XLA Ops:
  7.2 0.1 all-reduce.3.cloned.1.call-start
  7.3 38.1 %forward.1.h_ref = bf16[4096,512]{1,0:T(8,128)(2,1)} custom-call(bf16[4096,512]{1,0:T(8,128)(2,1)} %bitcast.2, bf16[2,512,2048]{2,1,0:T(8,128)(2,1)} %refs_0_.3, bf16[2,512,2048]{2,1,0:T(8,128)(2,1)} %refs_1_.3, bf16[2,2048,512]{2,1,0:T(8,128)(2,1)} %refs_2_.3), custom_call_target="tpu_custom_call" | custom-call | flops 25769803776 | tf_op jit(solution)/shard_map/forward/pallas_call | solution.py:226
  45.3 96.1 %last_layer.1 = (f32[4096,512]{1,0:T(8,128)}, bf16[8,1536,256]{2,1,0:T(8,128)(2,1)}) custom-call(bf16[4096,512]{1,0:T(8,128)(2,1)} %forward.1.h_ref, bf16[4096,512]{1,0:T(8,128)(2,1)} %bitcast.4, bf16[2,512,2048]{2,1,0:T(8,128)(2,1)} %refs_0_.3, bf16[2,512,2048]{2,1,0:T(8,128)(2,1)} %refs_1_.3, bf16[2,2048,512]{2,1,0:T(8,128)(2,1)} %refs_2_.3), custom_call_target="tpu_custom_call" | custom-call | flops 68719476736 | tf_op jit(solution)/shard_map/last_layer/pallas_call | solution.py:236
  141.5 0.1 all-reduce.3.cloned.1.call-update
  141.5 0.2 all-reduce.5.cloned.1.call-start
  141.8 81.5 %first_layer.1 = bf16[8,1536,256]{2,1,0:T(8,128)(2,1)} custom-call(bf16[4096,512]{1,0:T(8,128)(2,1)} %bitcast.3, bf16[4096,512]{1,0:T(8,128)(2,1)} %forward.1.h_ref, bf16[4096,512]{1,0:T(8,128)(2,1)} %bitcast.5, f32[4096,512]{1,0:T(8,128)} %get-tuple-element.22.da_ref, bf16[2,512,2048]{2,1,0:T(8,128)(2,1)} %refs_0_.3, bf16[2,512,2048]{2,1,0:T(8,128)(2,1)} %refs_1_.3, ...), custom_call_target="tpu_custom_call" | custom-call | flops 51539607552 | tf_op jit(solution)/shard_map/first_layer/pallas_call | solution.py:247
  223.3 64.5 %all-reduce.3.cloned.1.call-done.g_ref = bf16[8,1536,256]{2,1,0:T(8,128)(2,1)} async-done(((bf16[8,1536,256]{2,1,0:T(8,128)(2,1)}), bf16[8,1536,256]{2,1,0:T(8,128)(2,1)}) %all-reduce.3.cloned.1.call-update) | async-done | bytes 6291472 | tf_op jit(solution)/shard_map/psum | solution.py:246
  287.7 0.1 all-reduce.5.cloned.1.call-update
  287.8 0.0 copy-start
  287.8 2.2 copy-done
  290.0 0.0 copy-start.2
  290.0 2.2 copy-done.2
  292.2 0.0 copy-start.4
  292.2 2.2 copy-done.4
  294.4 23.0 %adam.2 = (bf16[2,512,2048]{2,1,0:T(8,128)(2,1)}, bf16[2,512,2048]{2,1,0:T(8,128)(2,1)}, bf16[2,2048,512]{2,1,0:T(8,128)(2,1)}, f32[2,512,2048]{2,1,0:T(8,128)},...) custom-call(bf16[8,1536,256]{2,1,0:T(8,128)(2,1)} %all-reduce.3.clon, ...), custom_call_target="tpu_custom_call" | custom-call | flops 62914560 | bytes 69206016 | tf_op jit(solution)/shard_map/adam/pallas_call | solution.py:198
  317.3 113.2 %all-reduce.5.cloned.1.call-done.g_ref = bf16[8,1536,256]{2,1,0:T(8,128)(2,1)} async-done(((bf16[8,1536,256]{2,1,0:T(8,128)(2,1)}), bf16[8,1536,256]{2,1,0:T(8,128)(2,1)}) %all-reduce.5.cloned.1.call-update) | async-done | bytes 6291472 | tf_op jit(solution)/shard_map/psum | solution.py:265
  430.6 0.0 copy-start.1
  430.6 2.2 copy-done.1
  432.8 0.0 copy-start.3
  432.8 2.2 copy-done.3
  435.0 0.0 copy-start.5
  435.0 2.2 copy-done.5
  437.1 23.3 %adam.3 = (bf16[2,512,2048]{2,1,0:T(8,128)(2,1)}, bf16[2,512,2048]{2,1,0:T(8,128)(2,1)}, bf16[2,2048,512]{2,1,0:T(8,128)(2,1)}, f32[2,512,2048]{2,1,0:T(8,128)},...) custom-call(bf16[8,1536,256]{2,1,0:T(8,128)(2,1)} %all-reduce.5.clon, ...), custom_call_target="tpu_custom_call", output_to_operand_aliasing={{0}: (10, {}), {1}: (11, {}), {2}: (12, {}), {3}: (13, {}),... | custom-call | flops 62914560 | bytes 69206016 | tf_op jit(solution)/shard_map/adam/pallas_call | solution.py:198
Async XLA Ops:
  7.2 280.6 %all-reduce.3.cloned.1.call-start = ((), (), s32[]{:S(2)}) async-start(), calls=%async_computation | async-start | bytes 12582912 | tf_op jit(solution)/shard_map/psum | solution.py:246
  141.5 289.0 %all-reduce.5.cloned.1.call-start = ((), (), s32[]{:S(2)}) async-start(), calls=%async_computation.1 | async-start | bytes 12582912 | tf_op jit(solution)/shard_map/psum | solution.py:265
  287.8 2.2 copy-start
  290.0 2.2 copy-start.2
  292.2 2.2 copy-start.4
  430.6 2.2 copy-start.1
  432.8 2.2 copy-start.3
  435.0 2.2 copy-start.5
Sparse Core Ops, SparseCore 0:
  141.7 146.0 all-reduce.2
  290.1 140.3 all-reduce.4
